TPU v7x, 128 devices: a whole 4x4x4 slice. The times are simulated.
128 devices in a mesh: var: 16 (over x, y), samp: 8 (over z, core).
Axes of the slice: x: 4, y: 4, z: 4, core: 2. Of those that a mesh axis runs over, the one named last changes fastest.
Arguments:
- dosage: int32 [24576, 8192], P('samp', 'var'), may hold values from 0 to 2, as said below
- phenotype: float32 [24576], P('samp'), may hold values from -6 to 6
- perm_index: int32 [1024, 24576], P('var', 'samp'), may hold values from 0 to 24575, each once within a row
- seg_lengths: int32 [128], replicated, may hold values from 1 to 128, 8192 in all
Outputs:
- zscore: float32 [1024, 8192], P('samp', 'var')
- thresholds: float32 [1024, 128], P('samp')
Inputs may be any that keep to these rules, and one draw needn't show every extreme that they name: `dosage`: each entry is an allele count. `perm_index`: each row is a permutation of the 24576 sample numbers. `seg_lengths`: the lengths sum to 8192, one of them equals 128.
All inputs are finite; a program needn't handle non-finite values.
Results may differ from a plain program's by a relative error of at most 0.0039.
Values may be sent and summed in bfloat16 or wider, within the bound.
No kernel may reach another device: no remote copies, remote signals or barrier semaphores. Data moves between devices by JAX's collectives and lax.ppermute only.
A program may use at most 64 MiB of HBM per device.

v0:
```python
import math
import jax
import jax.numpy as jnp
from jax import lax
from jax.sharding import PartitionSpec as P

epsilon = 1e-05


def in_order(blocks, dim):
    blocks = jnp.moveaxis(blocks, 0, dim)
    shape = blocks.shape
    return blocks.reshape(*shape[:dim], shape[dim] * shape[dim + 1], *shape[dim + 2 :])


def sent_to_all(value, axis):
    count = lax.axis_size(axis)
    return lax.all_to_all(
        jnp.broadcast_to(value[None], (count, *value.shape)), axis, 0, 0, tiled=True
    )


def collect(value, axis, dim):
    return in_order(sent_to_all(value, axis), dim)


def taken_together(value, axis):
    return sent_to_all(value, axis).sum(axis=0)


def packed_total(arrays, axis):
    ends = [0]
    for a in arrays:
        ends.append(ends[-1] + a.size)
    subtotal = taken_together(jnp.concatenate([a.ravel() for a in arrays]), axis)
    return tuple((subtotal[b:e].reshape(a.shape) for a, b, e in zip(arrays, ends, ends[1:])))


def cut_along(value, dim, count):
    before, after = (value.shape[:dim], value.shape[dim + 1 :])
    return jnp.moveaxis(value.reshape(*before, count, -1, *after), dim, 0)


def sum_at_owner(value, axis, dim):
    count = lax.axis_size(axis)
    blocks = lax.all_to_all(cut_along(value, dim, count), axis, 0, 0, tiled=True)
    return jnp.sum(blocks, axis=0)


def of_everyone(value, axis):
    return sent_to_all(value, axis).max(axis=0)


def pick_traits(rounded, perm_index):
    count_all = rounded.shape[0]
    low_width = math.gcd(128, count_all)
    high_count = count_all // low_width
    table = rounded.reshape(high_count, low_width)
    flat_index = perm_index.reshape(-1)
    entries = flat_index.shape[0]
    block_size = math.gcd(entries, 16384)
    blocks = flat_index.reshape(entries // block_size, block_size)

    def one_block(index_block):
        high_part = index_block // low_width
        low_part = index_block % low_width
        high_iota = lax.broadcasted_iota(jnp.int32, (block_size, high_count), 1)
        selector = (high_part[:, None] == high_iota).astype(jnp.bfloat16)
        table_rows = jnp.dot(selector, table, preferred_element_type=jnp.float32)
        low_iota = lax.broadcasted_iota(jnp.int32, (block_size, low_width), 1)
        chosen = jnp.sum(jnp.where(low_part[:, None] == low_iota, table_rows, 0.0), axis=1)
        return chosen.astype(jnp.bfloat16)

    picked_all = lax.map(one_block, blocks)
    return picked_all.reshape(perm_index.shape)


def running_max(values):
    width = values.shape[1]
    offset = 1
    while offset < width:
        shifted = jnp.pad(values[:, : width - offset], ((0, 0), (offset, 0)))
        values = jnp.maximum(values, shifted)
        offset = offset * 2
    return values


def per_device(dosage, phenotype, perm_index, seg_lengths):
    pheno_all = collect(phenotype, "samp", 0)
    count_all = pheno_all.shape[0]
    centered = pheno_all - jnp.mean(pheno_all)
    pheno_var = jnp.mean(centered * centered)
    rounded = centered.astype(jnp.bfloat16)
    permuted = pick_traits(rounded, perm_index)
    allele_sum, allele_sq = packed_total(
        (
            jnp.sum(dosage, axis=0).astype(jnp.float32),
            jnp.sum(dosage * dosage, axis=0).astype(jnp.float32),
        ),
        "samp",
    )
    allele_var = allele_sq / count_all - (allele_sum / count_all) ** 2
    dosage_bf = dosage.astype(jnp.bfloat16)
    all_perms = lax.all_gather(permuted, "var", axis=0, tiled=True)
    score = sum_at_owner(
        jnp.dot(all_perms, dosage_bf, preferred_element_type=jnp.float32), "samp", 0
    )
    divisor = jnp.sqrt(count_all * (pheno_var + epsilon) * (allele_var + epsilon))
    zscore = score / divisor[None, :]
    local_prefix = running_max(jnp.abs(zscore))
    block_max = local_prefix[:, -1]
    block_maxima = collect(block_max[None, :], "var", 0)
    position = lax.broadcasted_iota(jnp.int32, block_maxima.shape, 0)
    before = jnp.max(jnp.where(position < lax.axis_index("var"), block_maxima, 0.0), axis=0)
    prefix = jnp.maximum(local_prefix, before[:, None])
    width = dosage.shape[1]
    segment_end = jnp.cumsum(seg_lengths) - 1
    local_end = segment_end - lax.axis_index("var") * width
    column_iota = lax.broadcasted_iota(jnp.int32, (width, local_end.shape[0]), 0)
    match = column_iota == local_end[None, :]
    picked = jnp.max(jnp.where(match[None, :, :], prefix[:, :, None], 0.0), axis=1)
    thresholds = of_everyone(picked, "var")
    return (zscore, thresholds)


def solution(mesh):
    return jax.shard_map(
        per_device,
        mesh=mesh,
        in_specs=(P("samp", "var"), P("samp"), P("var", "samp"), P()),
        out_specs=(P("samp", "var"), P("samp", None)),
        check_vma=False,
    )
```

profile of v0, /device:TPU:0, one launch (start us, length us, event | category | flops | bytes accessed | tf_op | source)
XLA Modules:
  0.0 239.6 jit_solution(4275792382053469606)
XLA Ops:
  7.2 1.4 broadcast_in_dim.69
  8.6 5.4 %all-to-all-start = ((f32[8,1,3072]{2,1,0:T(1,128)}), f32[8,1,3072]{2,1,0:T(1,128)S(1)}, u32[]{:S(2)}, u32[]{:S(2)}) async-start(f32[8,1,3072]{2,1,0:T(1,128)} %broadcast_in_dim.69), calls=%async_computation | async-start | bytes 196608 | tf_op jit(solution)/shard_map/all_to_all | solution.py:18
  14.0 1.5 reshape_reshape.3
  15.5 4.3 %all-to-all-done = f32[8,1,3072]{2,1,0:T(1,128)S(1)} async-done(((f32[8,1,3072]{2,1,0:T(1,128)}), f32[8,1,3072]{2,1,0:T(1,128)S(1)}, u32[]{:S(2)}, u32[]{:S(2)}) %all-to-all-start) | async-done | bytes 98336 | tf_op jit(solution)/shard_map/all_to_all | solution.py:18
  19.8 0.8 reduce_sum.66
  21.2 0.3 convert_reduce_fusion
  21.5 62.9 %while.12 = (s32[]{:T(128)}, bf16[12,16384]{1,0:T(8,128)(2,1)S(1)}, s32[12,16384]{1,0:T(8,128)S(1)}, bf16[192,128]{1,0:T(8,128)(2,1)S(1)}, s32[]{:T(128)}, /*index=5*/s32[]{:T(128)}) while((s32[]{:T(128)}, bf16[12,16384]{1,0:T(8,128)(2,1)S(1)}, s32[12,16384]{1,0:T(8,128)S(1)}, bf16[192,128]{1,0:T(8,128)(2,1)S(1)}, s32[]{:T(128)}, ...), condition=%wide.region_3.4_spmd, body=%wide.region_1.3_spmd.sunk | while | flops 815038464 | bytes 671821 | solution.py:74
  21.7 3.9 %fusion.13 = bf16[16384]{0:T(1024)(128)(2,1)S(1)} fusion(bf16[192,128]{1,0:T(8,128)(2,1)S(1)} %get-tuple-element.117, s32[16384]{0:T(1024)S(1)} %get-tuple-element.100, s32[16384]{0:T(1024)S(1)} %get-tuple-element.101), kind=kOutput, calls=%fused_computation.4.clone.1 | convolution fusion | flops 814727168 | bytes 212992 | tf_op jit(solution)/shard_map/while/body/eval_jaxpr/dot_general | solution.py:69
  25.6 1.1 dynamic_update_slice.8
  26.9 3.9 %fusion.13 = bf16[16384]{0:T(1024)(128)(2,1)S(1)} fusion(bf16[192,128]{1,0:T(8,128)(2,1)S(1)} %get-tuple-element.117, s32[16384]{0:T(1024)S(1)} %get-tuple-element.100, s32[16384]{0:T(1024)S(1)} %get-tuple-element.101), kind=kOutput, calls=%fused_computation.4.clone.1 | convolution fusion | flops 814727168 | bytes 212992 | tf_op jit(solution)/shard_map/while/body/eval_jaxpr/dot_general | solution.py:69
  30.9 1.1 dynamic_update_slice.8
  32.2 3.9 %fusion.13 = bf16[16384]{0:T(1024)(128)(2,1)S(1)} fusion(bf16[192,128]{1,0:T(8,128)(2,1)S(1)} %get-tuple-element.117, s32[16384]{0:T(1024)S(1)} %get-tuple-element.100, s32[16384]{0:T(1024)S(1)} %get-tuple-element.101), kind=kOutput, calls=%fused_computation.4.clone.1 | convolution fusion | flops 814727168 | bytes 212992 | tf_op jit(solution)/shard_map/while/body/eval_jaxpr/dot_general | solution.py:69
  36.1 1.1 dynamic_update_slice.8
  37.4 3.9 %fusion.13 = bf16[16384]{0:T(1024)(128)(2,1)S(1)} fusion(bf16[192,128]{1,0:T(8,128)(2,1)S(1)} %get-tuple-element.117, s32[16384]{0:T(1024)S(1)} %get-tuple-element.100, s32[16384]{0:T(1024)S(1)} %get-tuple-element.101), kind=kOutput, calls=%fused_computation.4.clone.1 | convolution fusion | flops 814727168 | bytes 212992 | tf_op jit(solution)/shard_map/while/body/eval_jaxpr/dot_general | solution.py:69
  41.3 1.1 dynamic_update_slice.8
  42.6 3.9 %fusion.13 = bf16[16384]{0:T(1024)(128)(2,1)S(1)} fusion(bf16[192,128]{1,0:T(8,128)(2,1)S(1)} %get-tuple-element.117, s32[16384]{0:T(1024)S(1)} %get-tuple-element.100, s32[16384]{0:T(1024)S(1)} %get-tuple-element.101), kind=kOutput, calls=%fused_computation.4.clone.1 | convolution fusion | flops 814727168 | bytes 212992 | tf_op jit(solution)/shard_map/while/body/eval_jaxpr/dot_general | solution.py:69
  46.6 1.1 dynamic_update_slice.8
  47.9 3.9 %fusion.13 = bf16[16384]{0:T(1024)(128)(2,1)S(1)} fusion(bf16[192,128]{1,0:T(8,128)(2,1)S(1)} %get-tuple-element.117, s32[16384]{0:T(1024)S(1)} %get-tuple-element.100, s32[16384]{0:T(1024)S(1)} %get-tuple-element.101), kind=kOutput, calls=%fused_computation.4.clone.1 | convolution fusion | flops 814727168 | bytes 212992 | tf_op jit(solution)/shard_map/while/body/eval_jaxpr/dot_general | solution.py:69
  51.8 1.1 dynamic_update_slice.8
  53.1 3.9 %fusion.13 = bf16[16384]{0:T(1024)(128)(2,1)S(1)} fusion(bf16[192,128]{1,0:T(8,128)(2,1)S(1)} %get-tuple-element.117, s32[16384]{0:T(1024)S(1)} %get-tuple-element.100, s32[16384]{0:T(1024)S(1)} %get-tuple-element.101), kind=kOutput, calls=%fused_computation.4.clone.1 | convolution fusion | flops 814727168 | bytes 212992 | tf_op jit(solution)/shard_map/while/body/eval_jaxpr/dot_general | solution.py:69
  57.1 1.1 dynamic_update_slice.8
  58.3 3.9 %fusion.13 = bf16[16384]{0:T(1024)(128)(2,1)S(1)} fusion(bf16[192,128]{1,0:T(8,128)(2,1)S(1)} %get-tuple-element.117, s32[16384]{0:T(1024)S(1)} %get-tuple-element.100, s32[16384]{0:T(1024)S(1)} %get-tuple-element.101), kind=kOutput, calls=%fused_computation.4.clone.1 | convolution fusion | flops 814727168 | bytes 212992 | tf_op jit(solution)/shard_map/while/body/eval_jaxpr/dot_general | solution.py:69
  62.3 1.1 dynamic_update_slice.8
  63.6 3.9 %fusion.13 = bf16[16384]{0:T(1024)(128)(2,1)S(1)} fusion(bf16[192,128]{1,0:T(8,128)(2,1)S(1)} %get-tuple-element.117, s32[16384]{0:T(1024)S(1)} %get-tuple-element.100, s32[16384]{0:T(1024)S(1)} %get-tuple-element.101), kind=kOutput, calls=%fused_computation.4.clone.1 | convolution fusion | flops 814727168 | bytes 212992 | tf_op jit(solution)/shard_map/while/body/eval_jaxpr/dot_general | solution.py:69
  67.5 1.1 dynamic_update_slice.8
  68.8 3.9 %fusion.13 = bf16[16384]{0:T(1024)(128)(2,1)S(1)} fusion(bf16[192,128]{1,0:T(8,128)(2,1)S(1)} %get-tuple-element.117, s32[16384]{0:T(1024)S(1)} %get-tuple-element.100, s32[16384]{0:T(1024)S(1)} %get-tuple-element.101), kind=kOutput, calls=%fused_computation.4.clone.1 | convolution fusion | flops 814727168 | bytes 212992 | tf_op jit(solution)/shard_map/while/body/eval_jaxpr/dot_general | solution.py:69
  72.8 1.1 dynamic_update_slice.8
  74.1 3.9 %fusion.13 = bf16[16384]{0:T(1024)(128)(2,1)S(1)} fusion(bf16[192,128]{1,0:T(8,128)(2,1)S(1)} %get-tuple-element.117, s32[16384]{0:T(1024)S(1)} %get-tuple-element.100, s32[16384]{0:T(1024)S(1)} %get-tuple-element.101), kind=kOutput, calls=%fused_computation.4.clone.1 | convolution fusion | flops 814727168 | bytes 212992 | tf_op jit(solution)/shard_map/while/body/eval_jaxpr/dot_general | solution.py:69
  78.0 1.1 dynamic_update_slice.8
  79.3 3.9 %fusion.13 = bf16[16384]{0:T(1024)(128)(2,1)S(1)} fusion(bf16[192,128]{1,0:T(8,128)(2,1)S(1)} %get-tuple-element.117, s32[16384]{0:T(1024)S(1)} %get-tuple-element.100, s32[16384]{0:T(1024)S(1)} %get-tuple-element.101), kind=kOutput, calls=%fused_computation.4.clone.1 | convolution fusion | flops 814727168 | bytes 212992 | tf_op jit(solution)/shard_map/while/body/eval_jaxpr/dot_general | solution.py:69
  83.2 1.1 dynamic_update_slice.8
  84.4 1.3 reshape.151
  85.8 3.5 %fusion.6 = (s32[512]{0:T(512)S(1)}, s32[512]{0:T(512)S(1)}) fusion(s32[3072,512]{1,0:T(8,128)} %param.6), kind=kLoop, calls=%fused_computation.38 | loop fusion | flops 4717568 | bytes 6295552 | tf_op jit(solution)/shard_map/reduce_sum | solution.py:97
  89.3 0.6 broadcast_in_dim.70
  90.0 3.3 %all-to-all-start.2 = ((f32[8,1,1024]{2,1,0:T(1,128)}), f32[8,1,1024]{2,1,0:T(1,128)S(1)}, u32[]{:S(2)}, u32[]{:S(2)}) async-start(f32[8,1,1024]{2,1,0:T(1,128)} %broadcast_in_dim.70), calls=%async_computation.2 | async-start | bytes 65536 | tf_op jit(solution)/shard_map/all_to_all | solution.py:18
  93.3 53.3 %all-gather.2.cloned.1.call-done = bf16[1024,3072]{1,0:T(8,128)(2,1)} async-done(((bf16[64,3072]{1,0:T(8,128)(2,1)}), bf16[1024,3072]{1,0:T(8,128)(2,1)}) %all-gather.2.cloned.1.call-update) | async-done | bytes 6291472 | tf_op jit(solution)/shard_map/all_gather | solution.py:104
  146.6 9.4 %fusion.4 = f32[1024,512]{1,0:T(8,128)} fusion(bf16[1024,3072]{1,0:T(8,128)(2,1)} %all-gather.2.cloned.1.call-done, s32[3072,512]{1,0:T(8,128)} %param.6), kind=kOutput, calls=%fused_computation.16 | convolution fusion | flops 3222798336 | bytes 14680064 | tf_op jit(solution)/shard_map/dot_general | solution.py:106
  155.9 4.4 %all-to-all-start.1 = ((f32[8,128,512]{2,1,0:T(8,128)}), f32[8,128,512]{2,1,0:T(8,128)S(1)}, u32[]{:S(2)}, u32[]{:S(2)}) async-start(f32[8,128,512]{2,1,0:T(8,128)} %bitcast.24), calls=%async_computation.1 | async-start | bytes 4194304 | tf_op jit(solution)/shard_map/all_to_all | solution.py:46
  160.9 0.8 multiply_reduce_fusion.1
  162.3 25.2 %all-to-all-done.1 = f32[8,128,512]{2,1,0:T(8,128)S(1)} async-done(((f32[8,128,512]{2,1,0:T(8,128)}), f32[8,128,512]{2,1,0:T(8,128)S(1)}, u32[]{:S(2)}, u32[]{:S(2)}) %all-to-all-start.1) | async-done | bytes 2097184 | tf_op jit(solution)/shard_map/all_to_all | solution.py:46
  187.5 0.2 reduce_sum.67
  188.9 0.2 slice_reduce_fusion
  189.1 0.6 broadcast_in_dim.73
  189.7 5.3 %all-to-all-start.3 = ((f32[16,1,128]{2,1,0:T(1,128)}), f32[16,1,128]{2,1,0:T(1,128)S(1)}, u32[]{:S(2)}, u32[]{:S(2)}) async-start(f32[16,1,128]{2,1,0:T(1,128)} %broadcast_in_dim.73), calls=%async_computation.3 | async-start | bytes 16384 | tf_op jit(solution)/shard_map/all_to_all | solution.py:18
  195.0 7.5 %all-to-all-done.3 = f32[16,1,128]{2,1,0:T(1,128)S(1)} async-done(((f32[16,1,128]{2,1,0:T(1,128)}), f32[16,1,128]{2,1,0:T(1,128)S(1)}, u32[]{:S(2)}, u32[]{:S(2)}) %all-to-all-start.3) | async-done | bytes 8224 | tf_op jit(solution)/shard_map/all_to_all | solution.py:18
  202.7 10.9 %select_reduce_fusion = f32[128,128]{1,0:T(8,128)S(1)} fusion(f32[128,512]{1,0:T(8,128)S(1)} %broadcast_maximum_fusion, pred[512,128]{1,0:T(8,128)(4,1)S(1)} %iota_compare_fusion.5), kind=kLoop, calls=%fused_computation.14 | loop fusion | flops 16760832 | bytes 393216 | tf_op jit(solution)/shard_map/reduce_max | solution.py:121
  213.7 18.4 %all_to_all.27 = f32[16,128,128]{2,1,0:T(8,128)S(1)} all-to-all(f32[16,128,128]{2,1,0:T(8,128)S(1)} %broadcast_in_dim.77), channel_id=1, replica_groups=mesh['var'=16,'samp'=8] {'var'}, dimensions={0} | all-to-all | bytes 2097152 | tf_op jit(solution)/shard_map/all_to_all | solution.py:18
  232.1 0.7 reduce_max.29
  (70 shorter events, 3.8 us)
Async XLA Ops:
  8.6 11.2 %all-to-all-start = ((f32[8,1,3072]{2,1,0:T(1,128)}), f32[8,1,3072]{2,1,0:T(1,128)S(1)}, u32[]{:S(2)}, u32[]{:S(2)}) async-start(f32[8,1,3072]{2,1,0:T(1,128)} %broadcast_in_dim.69), calls=%async_computation | async-start | bytes 196608 | tf_op jit(solution)/shard_map/all_to_all | solution.py:18
  14.0 132.6 %all-gather.2.cloned.1.call-start = ((), (), s32[]{:S(2)}) async-start(), calls=%async_computation.5 | async-start | bytes 6684672 | tf_op jit(solution)/shard_map/all_gather | solution.py:104
  90.0 66.0 %all-to-all-start.2 = ((f32[8,1,1024]{2,1,0:T(1,128)}), f32[8,1,1024]{2,1,0:T(1,128)S(1)}, u32[]{:S(2)}, u32[]{:S(2)}) async-start(f32[8,1,1024]{2,1,0:T(1,128)} %broadcast_in_dim.70), calls=%async_computation.2 | async-start | bytes 65536 | tf_op jit(solution)/shard_map/all_to_all | solution.py:18
  93.3 67.1 %copy-start.1 = (s32[128]{0:T(128)S(1)}, s32[128]{0:T(128)}, u32[]{:S(2)}) copy-start(s32[128]{0:T(128)} %param.9) | copy-start | bytes 1540
  155.9 31.6 %all-to-all-start.1 = ((f32[8,128,512]{2,1,0:T(8,128)}), f32[8,128,512]{2,1,0:T(8,128)S(1)}, u32[]{:S(2)}, u32[]{:S(2)}) async-start(f32[8,128,512]{2,1,0:T(8,128)} %bitcast.24), calls=%async_computation.1 | async-start | bytes 4194304 | tf_op jit(solution)/shard_map/all_to_all | solution.py:46
  187.8 45.0 %copy-start = (f32[128,512]{1,0:T(8,128)}, f32[128,512]{1,0:T(8,128)S(1)}, u32[]{:S(2)}) copy-start(f32[128,512]{1,0:T(8,128)S(1)} %get-tuple-element.70) | copy-start | bytes 786436
  189.7 12.8 %all-to-all-start.3 = ((f32[16,1,128]{2,1,0:T(1,128)}), f32[16,1,128]{2,1,0:T(1,128)S(1)}, u32[]{:S(2)}, u32[]{:S(2)}) async-start(f32[16,1,128]{2,1,0:T(1,128)} %broadcast_in_dim.73), calls=%async_computation.3 | async-start | bytes 16384 | tf_op jit(solution)/shard_map/all_to_all | solution.py:18
Sparse Core Ops, SparseCore 0:
  85.9 60.6 all-gather.1
where the time goes:
time: 240 us
  waiting for transfers between devices  90.2 us (38%)
  matrix products  56.2 us (23%)
  local copies, waits for them, and re-layouts  20.6 us (9%)
  other arithmetic  19.6 us (8%)
  starting transfers between devices  18.5 us (8%)
  blocking collectives  18.4 us (8%)
  between operations  15.6 us (6%)
    all_gather x1, waiting for transfers between devices, per_device(): all_perms = lax.all_gather(permuted, 'var', axis=0, tiled=True)  53.3 us
    dot_general x12, matrix products, one_block(): table_rows = jnp.dot(selector, table, preferred_element_type=jnp.float32)  46.8 us
    all_to_all x1, waiting for transfers between devices, sum_at_owner(): lax.all_to_all(cut_along(value, dim, count), axis, 0, 0, tiled=True)  25.2 us
    all_to_all x1, blocking collectives, sent_to_all(): lax.all_to_all(jnp.broadcast_to(value[None], (count, *value.shape)), axis...  18.4 us
    all_to_all x3, starting transfers between devices, sent_to_all(): lax.all_to_all(jnp.broadcast_to(value[None], (count, *value.shape)), axis...  14 us
    dynamic_update_slice x12, local copies, waits for them, and re-layouts, pick_traits(): picked_all = lax.map(one_block, blocks)  13.7 us
    all_to_all x3, waiting for transfers between devices, sent_to_all(): lax.all_to_all(jnp.broadcast_to(value[None], (count, *value.shape)), axis...  11.8 us
    reduce_max x1, other arithmetic, per_device(): jnp.max(jnp.where(match[None, :, :], prefix[:, :, None], 0.0), axis=1)  10.9 us
  transfers between devices with their start and end apart: 5, of which 4 were waited for; matrix products, arithmetic and copies ran while one was open for 7% of the time, Pallas kernels for 0%

commit v1 on v0

--- a/solution.py
+++ b/solution.py
@@ -5,6 +5,19 @@
 from jax.sharding import PartitionSpec as P
 
 epsilon = 1e-05
+
+
+def ring_gather(shard, axis, dim):
+    ways = lax.axis_size(axis)
+    up = [(d, (d + 1) % ways) for d in range(ways)]
+    down = [(d, (d - 1) % ways) for d in range(ways)]
+    earlier, later = ([shard], [shard])
+    for _ in range(ways // 2):
+        earlier.append(lax.ppermute(earlier[-1], axis, up))
+    for _ in range((ways - 1) // 2):
+        later.append(lax.ppermute(later[-1], axis, down))
+    line = jnp.concatenate([*earlier[::-1], *later[1:]], axis=dim)
+    return jnp.roll(line, (lax.axis_index(axis) - ways // 2) * shard.shape[dim], axis=dim)
 
 
 def in_order(blocks, dim):
@@ -101,7 +114,7 @@
     )
     allele_var = allele_sq / count_all - (allele_sum / count_all) ** 2
     dosage_bf = dosage.astype(jnp.bfloat16)
-    all_perms = lax.all_gather(permuted, "var", axis=0, tiled=True)
+    all_perms = ring_gather(permuted, "var", 0)
     score = sum_at_owner(
         jnp.dot(all_perms, dosage_bf, preferred_element_type=jnp.float32), "samp", 0
     )

time: 240 us -> 276 us (1.15)
  starting transfers between devices: 18.5 us -> 60.1 us
  between operations: 15.6 us -> 2.56 us
  local copies, waits for them, and re-layouts: 20.6 us -> 30.8 us
  matrix products: 56.2 us -> 51.6 us
    ppermute x0 -> x15, waiting for transfers between devices: none -> 54.7 us  [the longest x8 52 us: ring_gather(): earlier.append(lax.ppermute(earlier[-1], axis, up))]
    all_gather x1 -> x0, waiting for transfers between devices: 53.3 us -> none  [per_device(): all_perms = lax.all_gather(permuted, 'var', axis=0, tiled=True)]
    ppermute x0 -> x15, starting transfers between devices: none -> 39.2 us  [the longest x7 37.6 us: ring_gather(): later.append(lax.ppermute(later[-1], axis, down))]
    unnamed x4 -> x51, local copies, waits for them, and re-layouts: 0.01 us -> 10.9 us
    dot_general x1, matrix products: 9.36 us -> 4.77 us  [per_device(): jnp.dot(all_perms, dosage_bf, preferred_element_type=jnp.float32)]
  transfers between devices with their start and end apart: 5 -> 19, of which waited for: 4 -> 11; matrix products, arithmetic and copies ran while one was open for 7% -> 8% of each run, Pallas kernels for 0% -> 0%
where the time goes in v1:
time: 276 us; the launch traced here: 275 us
  waiting for transfers between devices  90.9 us (33%)
  starting transfers between devices  60.1 us (22%)
  matrix products  51.6 us (19%)
  local copies, waits for them, and re-layouts  30.8 us (11%)
  other arithmetic  20.4 us (7%)
  blocking collectives  18.4 us (7%)
    ppermute x8, waiting for transfers between devices, ring_gather(): earlier.append(lax.ppermute(earlier[-1], axis, up))  52 us
    dot_general x12, matrix products, one_block(): table_rows = jnp.dot(selector, table, preferred_element_type=jnp.float32)  46.8 us
    ppermute x7, starting transfers between devices, ring_gather(): later.append(lax.ppermute(later[-1], axis, down))  37.6 us
    all_to_all x1, waiting for transfers between devices, sum_at_owner(): lax.all_to_all(cut_along(value, dim, count), axis, 0, 0, tiled=True)  24.4 us
    all_to_all x1, blocking collectives, sent_to_all(): lax.all_to_all(jnp.broadcast_to(value[None], (count, *value.shape)), axis...  18.4 us
    all_to_all x3, starting transfers between devices, sent_to_all(): lax.all_to_all(jnp.broadcast_to(value[None], (count, *value.shape)), axis...  16.5 us
    dynamic_update_slice x12, local copies, waits for them, and re-layouts, pick_traits(): picked_all = lax.map(one_block, blocks)  13.7 us
    all_to_all x3, waiting for transfers between devices, sent_to_all(): lax.all_to_all(jnp.broadcast_to(value[None], (count, *value.shape)), axis...  11.8 us
  transfers between devices with their start and end apart: 19, of which 11 were waited for; matrix products, arithmetic and copies ran while one was open for 8% of the time, Pallas kernels for 0%

profile of v1, /device:TPU:0, one launch (start us, length us, event | category | flops | bytes accessed | tf_op | source)
XLA Modules:
  0.0 275.3 jit_solution(13606035295653352563)
XLA Ops:
  0.6 1.4 broadcast_in_dim.69
  2.0 5.4 %all-to-all-start = ((f32[8,1,3072]{2,1,0:T(1,128)}), f32[8,1,3072]{2,1,0:T(1,128)S(1)}, u32[]{:S(2)}, u32[]{:S(2)}) async-start(f32[8,1,3072]{2,1,0:T(1,128)} %broadcast_in_dim.69), calls=%async_computation | async-start | bytes 196608 | tf_op jit(solution)/shard_map/all_to_all | solution.py:31
  7.5 1.5 reshape_reshape.3
  8.9 4.3 %all-to-all-done = f32[8,1,3072]{2,1,0:T(1,128)S(1)} async-done(((f32[8,1,3072]{2,1,0:T(1,128)}), f32[8,1,3072]{2,1,0:T(1,128)S(1)}, u32[]{:S(2)}, u32[]{:S(2)}) %all-to-all-start) | async-done | bytes 98336 | tf_op jit(solution)/shard_map/all_to_all | solution.py:31
  15.1 62.9 %while.12 = (s32[]{:T(128)}, bf16[12,16384]{1,0:T(8,128)(2,1)S(1)}, s32[12,16384]{1,0:T(8,128)S(1)}, bf16[192,128]{1,0:T(8,128)(2,1)S(1)}, s32[]{:T(128)}, /*index=5*/s32[]{:T(128)}) while((s32[]{:T(128)}, bf16[12,16384]{1,0:T(8,128)(2,1)S(1)}, s32[12,16384]{1,0:T(8,128)S(1)}, bf16[192,128]{1,0:T(8,128)(2,1)S(1)}, s32[]{:T(128)}, ...), condition=%wide.region_3.4_spmd, body=%wide.region_1.3_spmd.sunk | while | flops 815038464 | bytes 671829 | solution.py:87
  15.3 3.9 %fusion.14 = bf16[16384]{0:T(1024)(128)(2,1)S(1)} fusion(bf16[192,128]{1,0:T(8,128)(2,1)S(1)} %get-tuple-element.117, s32[16384]{0:T(1024)S(1)} %get-tuple-element.100, s32[16384]{0:T(1024)S(1)} %get-tuple-element.101), kind=kOutput, calls=%fused_computation.4.clone.1 | convolution fusion | flops 814727168 | bytes 212992 | tf_op jit(solution)/shard_map/while/body/eval_jaxpr/dot_general | solution.py:82
  19.2 1.1 dynamic_update_slice.8
  20.5 3.9 %fusion.14 = bf16[16384]{0:T(1024)(128)(2,1)S(1)} fusion(bf16[192,128]{1,0:T(8,128)(2,1)S(1)} %get-tuple-element.117, s32[16384]{0:T(1024)S(1)} %get-tuple-element.100, s32[16384]{0:T(1024)S(1)} %get-tuple-element.101), kind=kOutput, calls=%fused_computation.4.clone.1 | convolution fusion | flops 814727168 | bytes 212992 | tf_op jit(solution)/shard_map/while/body/eval_jaxpr/dot_general | solution.py:82
  24.5 1.1 dynamic_update_slice.8
  25.8 3.9 %fusion.14 = bf16[16384]{0:T(1024)(128)(2,1)S(1)} fusion(bf16[192,128]{1,0:T(8,128)(2,1)S(1)} %get-tuple-element.117, s32[16384]{0:T(1024)S(1)} %get-tuple-element.100, s32[16384]{0:T(1024)S(1)} %get-tuple-element.101), kind=kOutput, calls=%fused_computation.4.clone.1 | convolution fusion | flops 814727168 | bytes 212992 | tf_op jit(solution)/shard_map/while/body/eval_jaxpr/dot_general | solution.py:82
  29.7 1.1 dynamic_update_slice.8
  31.0 3.9 %fusion.14 = bf16[16384]{0:T(1024)(128)(2,1)S(1)} fusion(bf16[192,128]{1,0:T(8,128)(2,1)S(1)} %get-tuple-element.117, s32[16384]{0:T(1024)S(1)} %get-tuple-element.100, s32[16384]{0:T(1024)S(1)} %get-tuple-element.101), kind=kOutput, calls=%fused_computation.4.clone.1 | convolution fusion | flops 814727168 | bytes 212992 | tf_op jit(solution)/shard_map/while/body/eval_jaxpr/dot_general | solution.py:82
  36.2 3.9 %fusion.14 = bf16[16384]{0:T(1024)(128)(2,1)S(1)} fusion(bf16[192,128]{1,0:T(8,128)(2,1)S(1)} %get-tuple-element.117, s32[16384]{0:T(1024)S(1)} %get-tuple-element.100, s32[16384]{0:T(1024)S(1)} %get-tuple-element.101), kind=kOutput, calls=%fused_computation.4.clone.1 | convolution fusion | flops 814727168 | bytes 212992 | tf_op jit(solution)/shard_map/while/body/eval_jaxpr/dot_general | solution.py:82
  40.2 1.1 dynamic_update_slice.8
  41.5 3.9 %fusion.14 = bf16[16384]{0:T(1024)(128)(2,1)S(1)} fusion(bf16[192,128]{1,0:T(8,128)(2,1)S(1)} %get-tuple-element.117, s32[16384]{0:T(1024)S(1)} %get-tuple-element.100, s32[16384]{0:T(1024)S(1)} %get-tuple-element.101), kind=kOutput, calls=%fused_computation.4.clone.1 | convolution fusion | flops 814727168 | bytes 212992 | tf_op jit(solution)/shard_map/while/body/eval_jaxpr/dot_general | solution.py:82
  45.4 1.1 dynamic_update_slice.8
  46.7 3.9 %fusion.14 = bf16[16384]{0:T(1024)(128)(2,1)S(1)} fusion(bf16[192,128]{1,0:T(8,128)(2,1)S(1)} %get-tuple-element.117, s32[16384]{0:T(1024)S(1)} %get-tuple-element.100, s32[16384]{0:T(1024)S(1)} %get-tuple-element.101), kind=kOutput, calls=%fused_computation.4.clone.1 | convolution fusion | flops 814727168 | bytes 212992 | tf_op jit(solution)/shard_map/while/body/eval_jaxpr/dot_general | solution.py:82
  50.7 1.1 dynamic_update_slice.8
  51.9 3.9 %fusion.14 = bf16[16384]{0:T(1024)(128)(2,1)S(1)} fusion(bf16[192,128]{1,0:T(8,128)(2,1)S(1)} %get-tuple-element.117, s32[16384]{0:T(1024)S(1)} %get-tuple-element.100, s32[16384]{0:T(1024)S(1)} %get-tuple-element.101), kind=kOutput, calls=%fused_computation.4.clone.1 | convolution fusion | flops 814727168 | bytes 212992 | tf_op jit(solution)/shard_map/while/body/eval_jaxpr/dot_general | solution.py:82
  57.2 3.9 %fusion.14 = bf16[16384]{0:T(1024)(128)(2,1)S(1)} fusion(bf16[192,128]{1,0:T(8,128)(2,1)S(1)} %get-tuple-element.117, s32[16384]{0:T(1024)S(1)} %get-tuple-element.100, s32[16384]{0:T(1024)S(1)} %get-tuple-element.101), kind=kOutput, calls=%fused_computation.4.clone.1 | convolution fusion | flops 814727168 | bytes 212992 | tf_op jit(solution)/shard_map/while/body/eval_jaxpr/dot_general | solution.py:82
  62.4 3.9 %fusion.14 = bf16[16384]{0:T(1024)(128)(2,1)S(1)} fusion(bf16[192,128]{1,0:T(8,128)(2,1)S(1)} %get-tuple-element.117, s32[16384]{0:T(1024)S(1)} %get-tuple-element.100, s32[16384]{0:T(1024)S(1)} %get-tuple-element.101), kind=kOutput, calls=%fused_computation.4.clone.1 | convolution fusion | flops 814727168 | bytes 212992 | tf_op jit(solution)/shard_map/while/body/eval_jaxpr/dot_general | solution.py:82
  67.7 3.9 %fusion.14 = bf16[16384]{0:T(1024)(128)(2,1)S(1)} fusion(bf16[192,128]{1,0:T(8,128)(2,1)S(1)} %get-tuple-element.117, s32[16384]{0:T(1024)S(1)} %get-tuple-element.100, s32[16384]{0:T(1024)S(1)} %get-tuple-element.101), kind=kOutput, calls=%fused_computation.4.clone.1 | convolution fusion | flops 814727168 | bytes 212992 | tf_op jit(solution)/shard_map/while/body/eval_jaxpr/dot_general | solution.py:82
  72.9 3.9 %fusion.14 = bf16[16384]{0:T(1024)(128)(2,1)S(1)} fusion(bf16[192,128]{1,0:T(8,128)(2,1)S(1)} %get-tuple-element.117, s32[16384]{0:T(1024)S(1)} %get-tuple-element.100, s32[16384]{0:T(1024)S(1)} %get-tuple-element.101), kind=kOutput, calls=%fused_computation.4.clone.1 | convolution fusion | flops 814727168 | bytes 212992 | tf_op jit(solution)/shard_map/while/body/eval_jaxpr/dot_general | solution.py:82
  78.6 1.6 collective-permute-start
  80.2 12.6 %collective-permute-done = bf16[64,3072]{1,0:T(8,128)(2,1)S(1)} collective-permute-done((bf16[64,3072]{1,0:T(8,128)(2,1)S(1)}, bf16[64,3072]{1,0:T(8,128)(2,1)S(1)}, u32[]{:S(2)}, u32[]{:S(2)}) %collective-permute-start) | collective-permute-done | bytes 393248 | tf_op jit(solution)/shard_map/ppermute | solution.py:16
  92.8 5.3 %collective-permute-start.8 = (bf16[64,3072]{1,0:T(8,128)(2,1)S(1)}, bf16[64,3072]{1,0:T(8,128)(2,1)S(1)}, u32[]{:S(2)}, u32[]{:S(2)}) collective-permute-start(bf16[64,3072]{1,0:T(8,128)(2,1)S(1)} %reshape.151), channel_id=1, source_target_pairs={{0,120},{8,0},{16,8},{24,16},{32,24},{40,32},{48,40},{56,48},{64,5... | collective-permute-start | bytes 1179656 | tf_op jit(solution)/shard_map/ppermute | solution.py:18
  98.2 8.0 %collective-permute-done.1 = bf16[64,3072]{1,0:T(8,128)(2,1)S(1)} collective-permute-done((bf16[64,3072]{1,0:T(8,128)(2,1)S(1)}, bf16[64,3072]{1,0:T(8,128)(2,1)S(1)}, u32[]{:S(2)}, u32[]{:S(2)}) %collective-permute-start.1) | collective-permute-done | bytes 393248 | tf_op jit(solution)/shard_map/ppermute | solution.py:16
  106.1 5.3 %collective-permute-start.9 = (bf16[64,3072]{1,0:T(8,128)(2,1)S(1)}, bf16[64,3072]{1,0:T(8,128)(2,1)S(1)}, u32[]{:S(2)}, u32[]{:S(2)}) collective-permute-start(bf16[64,3072]{1,0:T(8,128)(2,1)S(1)} %collective-permute-done.8), channel_id=1, source_target_pairs={{0,120},{8,0},{16,8},{24,16},{32,24},{40,32},{48,40},{56,48},{64,5... | collective-permute-start | bytes 1179656 | tf_op jit(solution)/shard_map/ppermute | solution.py:18
  111.5 7.1 %collective-permute-done.2 = bf16[64,3072]{1,0:T(8,128)(2,1)S(1)} collective-permute-done((bf16[64,3072]{1,0:T(8,128)(2,1)S(1)}, bf16[64,3072]{1,0:T(8,128)(2,1)S(1)}, u32[]{:S(2)}, u32[]{:S(2)}) %collective-permute-start.2) | collective-permute-done | bytes 393248 | tf_op jit(solution)/shard_map/ppermute | solution.py:16
  118.6 5.3 %collective-permute-start.10 = (bf16[64,3072]{1,0:T(8,128)(2,1)S(1)}, bf16[64,3072]{1,0:T(8,128)(2,1)S(1)}, u32[]{:S(2)}, u32[]{:S(2)}) collective-permute-start(bf16[64,3072]{1,0:T(8,128)(2,1)S(1)} %collective-permute-done.9), channel_id=1, source_target_pairs={{0,120},{8,0},{16,8},{24,16},{32,24},{40,32},{48,40},{56,48},{64,5... | collective-permute-start | bytes 1179656 | tf_op jit(solution)/shard_map/ppermute | solution.py:18
  124.0 6.3 %collective-permute-done.3 = bf16[64,3072]{1,0:T(8,128)(2,1)S(1)} collective-permute-done((bf16[64,3072]{1,0:T(8,128)(2,1)S(1)}, bf16[64,3072]{1,0:T(8,128)(2,1)S(1)}, u32[]{:S(2)}, u32[]{:S(2)}) %collective-permute-start.3) | collective-permute-done | bytes 393248 | tf_op jit(solution)/shard_map/ppermute | solution.py:16
  130.2 5.3 %collective-permute-start.11 = (bf16[64,3072]{1,0:T(8,128)(2,1)S(1)}, bf16[64,3072]{1,0:T(8,128)(2,1)S(1)}, u32[]{:S(2)}, u32[]{:S(2)}) collective-permute-start(bf16[64,3072]{1,0:T(8,128)(2,1)S(1)} %collective-permute-done.10), channel_id=1, source_target_pairs={{0,120},{8,0},{16,8},{24,16},{32,24},{40,32},{48,40},{56,48},{64,5... | collective-permute-start | bytes 1179656 | tf_op jit(solution)/shard_map/ppermute | solution.py:18
  135.6 5.7 %collective-permute-done.4 = bf16[64,3072]{1,0:T(8,128)(2,1)S(1)} collective-permute-done((bf16[64,3072]{1,0:T(8,128)(2,1)S(1)}, bf16[64,3072]{1,0:T(8,128)(2,1)S(1)}, u32[]{:S(2)}, u32[]{:S(2)}) %collective-permute-start.4) | collective-permute-done | bytes 393248 | tf_op jit(solution)/shard_map/ppermute | solution.py:16
  141.3 5.3 %collective-permute-start.12 = (bf16[64,3072]{1,0:T(8,128)(2,1)S(1)}, bf16[64,3072]{1,0:T(8,128)(2,1)}, u32[]{:S(2)}, u32[]{:S(2)}) collective-permute-start(bf16[64,3072]{1,0:T(8,128)(2,1)S(1)} %collective-permute-done.11), channel_id=1, source_target_pairs={{0,120},{8,0},{16,8},{24,16},{32,24},{40,32},{48,40},{56,48},{64,5... | collective-permute-start | bytes 1179656 | tf_op jit(solution)/shard_map/ppermute | solution.py:18
  146.7 5.7 %collective-permute-done.5 = bf16[64,3072]{1,0:T(8,128)(2,1)S(1)} collective-permute-done((bf16[64,3072]{1,0:T(8,128)(2,1)S(1)}, bf16[64,3072]{1,0:T(8,128)(2,1)S(1)}, u32[]{:S(2)}, u32[]{:S(2)}) %collective-permute-start.5) | collective-permute-done | bytes 393248 | tf_op jit(solution)/shard_map/ppermute | solution.py:16
  152.4 5.4 %collective-permute-start.13 = (bf16[64,3072]{1,0:T(8,128)(2,1)}, bf16[64,3072]{1,0:T(8,128)(2,1)}, u32[]{:S(2)}, u32[]{:S(2)}) collective-permute-start(bf16[64,3072]{1,0:T(8,128)(2,1)} %collective-permute-done.12), channel_id=1, source_target_pairs={{0,120},{8,0},{16,8},{24,16},{32,24},{40,32},{48,40},{56,48},{64,5... | collective-permute-start | bytes 1179656 | tf_op jit(solution)/shard_map/ppermute | solution.py:18
  157.9 6.5 %collective-permute-done.6 = bf16[64,3072]{1,0:T(8,128)(2,1)} collective-permute-done((bf16[64,3072]{1,0:T(8,128)(2,1)S(1)}, bf16[64,3072]{1,0:T(8,128)(2,1)}, u32[]{:S(2)}, u32[]{:S(2)}) %collective-permute-start.6) | collective-permute-done | bytes 393248 | tf_op jit(solution)/shard_map/ppermute | solution.py:16
  164.4 3.5 %fusion.8 = (s32[512]{0:T(512)S(1)}, s32[512]{0:T(512)S(1)}) fusion(s32[3072,512]{1,0:T(8,128)} %param.6), kind=kLoop, calls=%fused_computation.72 | loop fusion | flops 4717568 | bytes 6295552 | tf_op jit(solution)/shard_map/reduce_sum | solution.py:110
  168.6 4.0 %all-to-all-start.2 = ((f32[8,1,1024]{2,1,0:T(1,128)}), f32[8,1,1024]{2,1,0:T(1,128)}, u32[]{:S(2)}, u32[]{:S(2)}) async-start(f32[8,1,1024]{2,1,0:T(1,128)} %broadcast_in_dim.70), calls=%async_computation.2 | async-start | bytes 65536 | tf_op jit(solution)/shard_map/all_to_all | solution.py:31
  172.6 5.4 %collective-permute-start.14 = (bf16[64,3072]{1,0:T(8,128)(2,1)}, bf16[64,3072]{1,0:T(8,128)(2,1)S(1)}, u32[]{:S(2)}, u32[]{:S(2)}) collective-permute-start(bf16[64,3072]{1,0:T(8,128)(2,1)} %collective-permute-done.13), channel_id=1, source_target_pairs={{0,120},{8,0},{16,8},{24,16},{32,24},{40,32},{48,40},{56,48},{64,5... | collective-permute-start | bytes 1179656 | tf_op jit(solution)/shard_map/ppermute | solution.py:18
  184.6 2.7 collective-permute-done.14
  191.9 4.8 %fusion.4 = f32[1024,512]{1,0:T(8,128)} fusion(bf16[2048,3072]{1,0:T(8,128)(2,1)S(1)} %constant_dynamic-update-slice_fusion, s32[]{:T(128)S(6)} %select_n.56, s32[3072,512]{1,0:T(8,128)S(1)} %bitcast.18), kind=kOutput, calls=%fused_computation.16 | convolution fusion | flops 3222798336 | bytes 14680068 | tf_op jit(solution)/shard_map/dot_general | solution.py:119
  196.6 4.4 %all-to-all-start.1 = ((f32[8,128,512]{2,1,0:T(8,128)}), f32[8,128,512]{2,1,0:T(8,128)S(1)}, u32[]{:S(2)}, u32[]{:S(2)}) async-start(f32[8,128,512]{2,1,0:T(8,128)} %bitcast.25), calls=%async_computation.1 | async-start | bytes 4194304 | tf_op jit(solution)/shard_map/all_to_all | solution.py:59
  203.8 24.4 %all-to-all-done.1 = f32[8,128,512]{2,1,0:T(8,128)S(1)} async-done(((f32[8,128,512]{2,1,0:T(8,128)}), f32[8,128,512]{2,1,0:T(8,128)S(1)}, u32[]{:S(2)}, u32[]{:S(2)}) %all-to-all-start.1) | async-done | bytes 2097184 | tf_op jit(solution)/shard_map/all_to_all | solution.py:59
  230.5 7.1 %all-to-all-start.3 = ((f32[16,1,128]{2,1,0:T(1,128)}), f32[16,1,128]{2,1,0:T(1,128)S(1)}, u32[]{:S(2)}, u32[]{:S(2)}) async-start(f32[16,1,128]{2,1,0:T(1,128)} %broadcast_in_dim.73), calls=%async_computation.3 | async-start | bytes 16384 | tf_op jit(solution)/shard_map/all_to_all | solution.py:31
  237.6 7.5 %all-to-all-done.3 = f32[16,1,128]{2,1,0:T(1,128)S(1)} async-done(((f32[16,1,128]{2,1,0:T(1,128)}), f32[16,1,128]{2,1,0:T(1,128)S(1)}, u32[]{:S(2)}, u32[]{:S(2)}) %all-to-all-start.3) | async-done | bytes 8224 | tf_op jit(solution)/shard_map/all_to_all | solution.py:31
  245.2 10.9 %select_reduce_fusion = f32[128,128]{1,0:T(8,128)S(1)} fusion(f32[128,512]{1,0:T(8,128)S(1)} %broadcast_maximum_fusion, pred[512,128]{1,0:T(8,128)(4,1)S(1)} %iota_compare_fusion.5), kind=kLoop, calls=%fused_computation.14 | loop fusion | flops 16760832 | bytes 393216 | tf_op jit(solution)/shard_map/reduce_max | solution.py:134
  256.3 18.4 %all_to_all.27 = f32[16,128,128]{2,1,0:T(8,128)S(1)} all-to-all(f32[16,128,128]{2,1,0:T(8,128)S(1)} %broadcast_in_dim.77), channel_id=1, replica_groups=mesh['var'=16,'samp'=8] {'var'}, dimensions={0} | all-to-all | bytes 2097152 | tf_op jit(solution)/shard_map/all_to_all | solution.py:31
  (146 shorter events, 27.1 us)
Async XLA Ops:
  2.0 11.2 %all-to-all-start = ((f32[8,1,3072]{2,1,0:T(1,128)}), f32[8,1,3072]{2,1,0:T(1,128)S(1)}, u32[]{:S(2)}, u32[]{:S(2)}) async-start(f32[8,1,3072]{2,1,0:T(1,128)} %broadcast_in_dim.69), calls=%async_computation | async-start | bytes 196608 | tf_op jit(solution)/shard_map/all_to_all | solution.py:31
  13.3 1.9 copy-start.4
  78.6 14.2 %collective-permute-start = (bf16[64,3072]{1,0:T(8,128)(2,1)S(1)}, bf16[64,3072]{1,0:T(8,128)(2,1)S(1)}, u32[]{:S(2)}, u32[]{:S(2)}) collective-permute-start(bf16[64,3072]{1,0:T(8,128)(2,1)S(1)} %reshape.151), channel_id=1, source_target_pairs={{0,8},{8,16},{16,24},{24,32},{32,40},{40,48},{48,56},{56,64},{64,7... | collective-permute-start | bytes 1179656 | tf_op jit(solution)/shard_map/ppermute | solution.py:16
  92.8 13.3 %collective-permute-start.1 = (bf16[64,3072]{1,0:T(8,128)(2,1)S(1)}, bf16[64,3072]{1,0:T(8,128)(2,1)S(1)}, u32[]{:S(2)}, u32[]{:S(2)}) collective-permute-start(bf16[64,3072]{1,0:T(8,128)(2,1)S(1)} %collective-permute-done), channel_id=1, source_target_pairs={{0,8},{8,16},{16,24},{24,32},{32,40},{40,48},{48,56},{56,64},{64,7... | collective-permute-start | bytes 1179656 | tf_op jit(solution)/shard_map/ppermute | solution.py:16
  92.8 13.3 %collective-permute-start.8 = (bf16[64,3072]{1,0:T(8,128)(2,1)S(1)}, bf16[64,3072]{1,0:T(8,128)(2,1)S(1)}, u32[]{:S(2)}, u32[]{:S(2)}) collective-permute-start(bf16[64,3072]{1,0:T(8,128)(2,1)S(1)} %reshape.151), channel_id=1, source_target_pairs={{0,120},{8,0},{16,8},{24,16},{32,24},{40,32},{48,40},{56,48},{64,5... | collective-permute-start | bytes 1179656 | tf_op jit(solution)/shard_map/ppermute | solution.py:18
  106.1 12.5 %collective-permute-start.2 = (bf16[64,3072]{1,0:T(8,128)(2,1)S(1)}, bf16[64,3072]{1,0:T(8,128)(2,1)S(1)}, u32[]{:S(2)}, u32[]{:S(2)}) collective-permute-start(bf16[64,3072]{1,0:T(8,128)(2,1)S(1)} %collective-permute-done.1), channel_id=1, source_target_pairs={{0,8},{8,16},{16,24},{24,32},{32,40},{40,48},{48,56},{56,64},{64,7... | collective-permute-start | bytes 1179656 | tf_op jit(solution)/shard_map/ppermute | solution.py:16
  106.1 12.5 %collective-permute-start.9 = (bf16[64,3072]{1,0:T(8,128)(2,1)S(1)}, bf16[64,3072]{1,0:T(8,128)(2,1)S(1)}, u32[]{:S(2)}, u32[]{:S(2)}) collective-permute-start(bf16[64,3072]{1,0:T(8,128)(2,1)S(1)} %collective-permute-done.8), channel_id=1, source_target_pairs={{0,120},{8,0},{16,8},{24,16},{32,24},{40,32},{48,40},{56,48},{64,5... | collective-permute-start | bytes 1179656 | tf_op jit(solution)/shard_map/ppermute | solution.py:18
  118.6 11.6 %collective-permute-start.3 = (bf16[64,3072]{1,0:T(8,128)(2,1)S(1)}, bf16[64,3072]{1,0:T(8,128)(2,1)S(1)}, u32[]{:S(2)}, u32[]{:S(2)}) collective-permute-start(bf16[64,3072]{1,0:T(8,128)(2,1)S(1)} %collective-permute-done.2), channel_id=1, source_target_pairs={{0,8},{8,16},{16,24},{24,32},{32,40},{40,48},{48,56},{56,64},{64,7... | collective-permute-start | bytes 1179656 | tf_op jit(solution)/shard_map/ppermute | solution.py:16
  118.6 11.6 %collective-permute-start.10 = (bf16[64,3072]{1,0:T(8,128)(2,1)S(1)}, bf16[64,3072]{1,0:T(8,128)(2,1)S(1)}, u32[]{:S(2)}, u32[]{:S(2)}) collective-permute-start(bf16[64,3072]{1,0:T(8,128)(2,1)S(1)} %collective-permute-done.9), channel_id=1, source_target_pairs={{0,120},{8,0},{16,8},{24,16},{32,24},{40,32},{48,40},{56,48},{64,5... | collective-permute-start | bytes 1179656 | tf_op jit(solution)/shard_map/ppermute | solution.py:18
  130.2 11.1 %collective-permute-start.4 = (bf16[64,3072]{1,0:T(8,128)(2,1)S(1)}, bf16[64,3072]{1,0:T(8,128)(2,1)S(1)}, u32[]{:S(2)}, u32[]{:S(2)}) collective-permute-start(bf16[64,3072]{1,0:T(8,128)(2,1)S(1)} %collective-permute-done.3), channel_id=1, source_target_pairs={{0,8},{8,16},{16,24},{24,32},{32,40},{40,48},{48,56},{56,64},{64,7... | collective-permute-start | bytes 1179656 | tf_op jit(solution)/shard_map/ppermute | solution.py:16
  130.2 11.1 %collective-permute-start.11 = (bf16[64,3072]{1,0:T(8,128)(2,1)S(1)}, bf16[64,3072]{1,0:T(8,128)(2,1)S(1)}, u32[]{:S(2)}, u32[]{:S(2)}) collective-permute-start(bf16[64,3072]{1,0:T(8,128)(2,1)S(1)} %collective-permute-done.10), channel_id=1, source_target_pairs={{0,120},{8,0},{16,8},{24,16},{32,24},{40,32},{48,40},{56,48},{64,5... | collective-permute-start | bytes 1179656 | tf_op jit(solution)/shard_map/ppermute | solution.py:18
  141.3 11.1 %copy-start = (bf16[64,3072]{1,0:T(8,128)(2,1)}, bf16[64,3072]{1,0:T(8,128)(2,1)S(1)}, u32[]{:S(2)}) copy-start(bf16[64,3072]{1,0:T(8,128)(2,1)S(1)} %collective-permute-done.4) | copy-start | bytes 1179652
  141.3 11.1 %collective-permute-start.5 = (bf16[64,3072]{1,0:T(8,128)(2,1)S(1)}, bf16[64,3072]{1,0:T(8,128)(2,1)S(1)}, u32[]{:S(2)}, u32[]{:S(2)}) collective-permute-start(bf16[64,3072]{1,0:T(8,128)(2,1)S(1)} %collective-permute-done.4), channel_id=1, source_target_pairs={{0,8},{8,16},{16,24},{24,32},{32,40},{40,48},{48,56},{56,64},{64,7... | collective-permute-start | bytes 1179656 | tf_op jit(solution)/shard_map/ppermute | solution.py:16
  141.3 11.1 %collective-permute-start.12 = (bf16[64,3072]{1,0:T(8,128)(2,1)S(1)}, bf16[64,3072]{1,0:T(8,128)(2,1)}, u32[]{:S(2)}, u32[]{:S(2)}) collective-permute-start(bf16[64,3072]{1,0:T(8,128)(2,1)S(1)} %collective-permute-done.11), channel_id=1, source_target_pairs={{0,120},{8,0},{16,8},{24,16},{32,24},{40,32},{48,40},{56,48},{64,5... | collective-permute-start | bytes 1179656 | tf_op jit(solution)/shard_map/ppermute | solution.py:18
  152.4 5.5 %copy-start.2 = (bf16[64,3072]{1,0:T(8,128)(2,1)}, bf16[64,3072]{1,0:T(8,128)(2,1)S(1)}, u32[]{:S(2)}) copy-start(bf16[64,3072]{1,0:T(8,128)(2,1)S(1)} %collective-permute-done.5) | copy-start | bytes 1179652
  152.4 12.0 %collective-permute-start.6 = (bf16[64,3072]{1,0:T(8,128)(2,1)S(1)}, bf16[64,3072]{1,0:T(8,128)(2,1)}, u32[]{:S(2)}, u32[]{:S(2)}) collective-permute-start(bf16[64,3072]{1,0:T(8,128)(2,1)S(1)} %collective-permute-done.5), channel_id=1, source_target_pairs={{0,8},{8,16},{16,24},{24,32},{32,40},{40,48},{48,56},{56,64},{64,7... | collective-permute-start | bytes 1179656 | tf_op jit(solution)/shard_map/ppermute | solution.py:16
  152.4 20.2 %collective-permute-start.13 = (bf16[64,3072]{1,0:T(8,128)(2,1)}, bf16[64,3072]{1,0:T(8,128)(2,1)}, u32[]{:S(2)}, u32[]{:S(2)}) collective-permute-start(bf16[64,3072]{1,0:T(8,128)(2,1)} %collective-permute-done.12), channel_id=1, source_target_pairs={{0,120},{8,0},{16,8},{24,16},{32,24},{40,32},{48,40},{56,48},{64,5... | collective-permute-start | bytes 1179656 | tf_op jit(solution)/shard_map/ppermute | solution.py:18
  164.4 13.6 %collective-permute-start.7 = (bf16[64,3072]{1,0:T(8,128)(2,1)}, bf16[64,3072]{1,0:T(8,128)(2,1)}, u32[]{:S(2)}, u32[]{:S(2)}) collective-permute-start(bf16[64,3072]{1,0:T(8,128)(2,1)} %collective-permute-done.6), channel_id=1, source_target_pairs={{0,8},{8,16},{16,24},{24,32},{32,40},{40,48},{48,56},{56,64},{64,7... | collective-permute-start | bytes 1179656 | tf_op jit(solution)/shard_map/ppermute | solution.py:16
  168.6 28.0 %all-to-all-start.2 = ((f32[8,1,1024]{2,1,0:T(1,128)}), f32[8,1,1024]{2,1,0:T(1,128)}, u32[]{:S(2)}, u32[]{:S(2)}) async-start(f32[8,1,1024]{2,1,0:T(1,128)} %broadcast_in_dim.70), calls=%async_computation.2 | async-start | bytes 65536 | tf_op jit(solution)/shard_map/all_to_all | solution.py:31
  172.6 16.7 %copy-start.3 = (bf16[64,3072]{1,0:T(8,128)(2,1)S(1)}, bf16[64,3072]{1,0:T(8,128)(2,1)}, u32[]{:S(2)}) copy-start(bf16[64,3072]{1,0:T(8,128)(2,1)} %copy-done.2) | copy-start | bytes 1179652
  172.6 16.8 %copy-start.1 = (bf16[64,3072]{1,0:T(8,128)(2,1)S(1)}, bf16[64,3072]{1,0:T(8,128)(2,1)}, u32[]{:S(2)}) copy-start(bf16[64,3072]{1,0:T(8,128)(2,1)} %copy-done) | copy-start | bytes 1179652
  172.6 19.2 %slice-start = ((s8[6291456]{0:T(1024)(128)(4,1)}), s8[4194304]{0:T(1024)(128)(4,1)S(1)}, s32[]{:S(2)}) async-start(s8[6291456]{0:T(1024)(128)(4,1)} %bitcast.17), calls=%async_computation.5 | async-start | bytes 8388608
  172.6 14.6 %collective-permute-start.14 = (bf16[64,3072]{1,0:T(8,128)(2,1)}, bf16[64,3072]{1,0:T(8,128)(2,1)S(1)}, u32[]{:S(2)}, u32[]{:S(2)}) collective-permute-start(bf16[64,3072]{1,0:T(8,128)(2,1)} %collective-permute-done.13), channel_id=1, source_target_pairs={{0,120},{8,0},{16,8},{24,16},{32,24},{40,32},{48,40},{56,48},{64,5... | collective-permute-start | bytes 1179656 | tf_op jit(solution)/shard_map/ppermute | solution.py:18
  184.5 7.3 %slice-start.1 = ((s8[6291456]{0:T(1024)(128)(4,1)}), s8[2097152]{0:T(1024)(128)(4,1)S(1)}, s32[]{:S(2)}) async-start(s8[6291456]{0:T(1024)(128)(4,1)} %bitcast.17), calls=%async_computation.6 | async-start | bytes 4194304
  191.9 9.2 %copy-start.7 = (s32[128]{0:T(128)S(1)}, s32[128]{0:T(128)}, u32[]{:S(2)}) copy-start(s32[128]{0:T(128)} %param.9) | copy-start | bytes 1540
  191.9 10.5 %copy-start.5 = (f32[8,1,3072]{2,1,0:T(1,128)S(1)}, f32[8,1,3072]{2,1,0:T(1,128)}, u32[]{:S(2)}) copy-start(f32[8,1,3072]{2,1,0:T(1,128)} %copy-done.4) | copy-start | bytes 294916
  196.6 31.6 %all-to-all-start.1 = ((f32[8,128,512]{2,1,0:T(8,128)}), f32[8,128,512]{2,1,0:T(8,128)S(1)}, u32[]{:S(2)}, u32[]{:S(2)}) async-start(f32[8,128,512]{2,1,0:T(8,128)} %bitcast.25), calls=%async_computation.1 | async-start | bytes 4194304 | tf_op jit(solution)/shard_map/all_to_all | solution.py:59
  228.5 46.8 %copy-start.6 = (f32[128,512]{1,0:T(8,128)}, f32[128,512]{1,0:T(8,128)S(1)}, u32[]{:S(2)}) copy-start(f32[128,512]{1,0:T(8,128)S(1)} %get-tuple-element.70) | copy-start | bytes 786436
  230.5 14.6 %all-to-all-start.3 = ((f32[16,1,128]{2,1,0:T(1,128)}), f32[16,1,128]{2,1,0:T(1,128)S(1)}, u32[]{:S(2)}, u32[]{:S(2)}) async-start(f32[16,1,128]{2,1,0:T(1,128)} %broadcast_in_dim.73), calls=%async_computation.3 | async-start | bytes 16384 | tf_op jit(solution)/shard_map/all_to_all | solution.py:31
